TPU v7x, 512 devices: a whole 4x4x16 slice. The times are simulated.
512 devices in a mesh: lag: 4 (over x_hi, core), row: 32 (over z, x_lo), col: 4 (over y).
Axes of the slice: x: 4 (x_hi: 2, x_lo: 2; x = x_hi * 2 + x_lo), y: 4, z: 16, core: 2. Of those that a mesh axis runs over, the one named last changes fastest.
Arguments:
- impedance: bfloat16 [4, 12288, 12288], P('lag', 'row', 'col'), may hold values from -0.013671875 to 0.013671875
- history: bfloat16 [4, 4, 32, 96, 128], P('lag', 'col', 'row'), may hold values from -6 to 6
- excitation: float32 [2, 32, 16, 24, 128], P(None, 'row', ('lag', 'col')), may hold values from -6 to 6
- inv_self: float32 [12288], P('row'), may hold values from 0.4 to 1.2
- cubic_coef: float32 [12288], P('row'), may hold values from 0.01 to 0.1
Outputs:
- currents: float32 [2, 32, 16, 24, 128], P(None, 'row', ('lag', 'col'))
All inputs are finite; a program needn't handle non-finite values.
Results may differ from a plain program's by a relative error of at most 0.00054.
Values may be sent and summed in bfloat16 or wider, within the bound.
No kernel may reach another device: no remote copies, remote signals or barrier semaphores. Data moves between devices by JAX's collectives and lax.ppermute only.
A program may use at most 64 MiB of HBM per device.

v0:
```python
import jax
import jax.numpy as jnp
from jax import lax
from jax.sharding import Mesh
from jax.sharding import PartitionSpec as P

STEPS = 2
ROW = ("row_0", "row_1")


def gather_axes(x, axes, dim):
    for axis in reversed(axes):
        x = lax.all_gather(x, axis, axis=dim, tiled=True)
    return x


def picked(x, axis, root):
    return lax.dynamic_index_in_dim(lax.all_gather(x, axis), root, 0, keepdims=False)


def in_blocks(x, dim, size):
    dims = x.shape
    blocks = x.reshape(*dims[:dim], size, dims[dim] // size, *dims[dim + 1 :])
    return jnp.moveaxis(blocks, dim, 0)


def sum_at_owner(x, axis, dim):
    blocks = in_blocks(x, dim, lax.axis_size(axis))
    arrived = lax.all_to_all(blocks, axis, split_axis=0, concat_axis=0, tiled=True)
    return arrived.sum(axis=0)


def joined_along(blocks, dim):
    blocks = jnp.moveaxis(blocks, 0, dim)
    dims = blocks.shape
    return blocks.reshape(*dims[:dim], dims[dim] * dims[dim + 1], *dims[dim + 2 :])


def sent_to_all(x, axis):
    copies = jnp.broadcast_to(x, (lax.axis_size(axis), *x.shape))
    return lax.all_to_all(copies, axis, split_axis=0, concat_axis=0, tiled=True)


def collect(x, axis, dim):
    return joined_along(sent_to_all(x, axis), dim)


def shifted_2(value, axis, steps):
    count = lax.axis_size(axis)
    first, last = (max(0, -steps), min(count, count - steps))
    return lax.ppermute(value, axis, [(source, source + steps) for source in range(first, last)])


def update(residual, inv_rows, coef_rows):
    scaled = residual * inv_rows[:, None]
    return scaled + coef_rows[:, None] * scaled * scaled * scaled


def shards(impedance, history, excitation, inv_self, cubic_coef):
    lag_index = lax.axis_index("lag")
    col_index = lax.axis_index("col")
    col_count = lax.axis_size("col")
    local_lags = impedance.shape[0]
    rb_rows = impedance.shape[1]
    cb_rows = impedance.shape[2]
    width = history.shape[-1]
    share_rows = excitation.shape[3]
    share_index = lag_index * col_count + col_index
    offset = share_index * share_rows
    root_count = max(1, cb_rows // rb_rows)
    stored = gather_axes(history, ROW, 2).reshape(local_lags, cb_rows, width)
    window = [stored[0]]
    results = []
    for moment in range(STEPS):
        product = jnp.dot(impedance[0], window[0], preferred_element_type=jnp.float32)
        contrib = -product
        own_rows = (
            lax.dynamic_slice_in_dim(contrib, offset, share_rows, 0) + excitation[moment, 0, 0]
        )
        contrib = lax.dynamic_update_slice_in_dim(contrib, own_rows, offset, 0)
        owned_block = None
        owned = sum_at_owner(contrib, ("lag", "col"), 0)
        inv_rows = lax.dynamic_slice_in_dim(inv_self, offset, share_rows, 0)
        coef_rows = lax.dynamic_slice_in_dim(cubic_coef, offset, share_rows, 0)
        new_share = update(owned, inv_rows, coef_rows)
        results.append(new_share)
        if moment + 1 < STEPS:
            owned_block = collect(new_share.astype(jnp.bfloat16), ("lag", "col"), 0)
        if moment + 1 < STEPS:
            received = []
            for number in range(root_count):
                source_root = col_index * cb_rows // rb_rows + number
                received.append(picked(owned_block, ROW, source_root))
            full_block = jnp.concatenate(received, 0)
            shifted = shifted_2(window[local_lags - 1], "lag", 1)
            first = jnp.where(lag_index == 0, full_block, shifted)
            window = [first] + window[: local_lags - 1]
    return jnp.stack(results)[:, None, None]


def solution(mesh):
    split = Mesh(
        mesh.devices.reshape(mesh.shape["lag"], 16, 2, mesh.shape["col"]),
        ("lag", "row_0", "row_1", "col"),
    )
    in_specs = (
        P("lag", ROW, "col"),
        P("lag", "col", ROW, None, None),
        P(None, ROW, ("lag", "col"), None, None),
        P(ROW),
        P(ROW),
    )
    out_specs = P(None, ROW, ("lag", "col"), None, None)
    return jax.shard_map(
        shards, mesh=split, in_specs=in_specs, out_specs=out_specs, check_vma=False
    )
```

profile of v0, /device:TPU:1, one launch (start us, length us, event | category | flops | bytes accessed | tf_op | source)
XLA Modules:
  0.0 243.4 jit_solution(5057360695156447709)
XLA Ops:
  6.5 4.3 %all_gather.6 = bf16[1,1,2,96,128]{4,3,1,0,2:T(8,128)(2,1)S(1)} all-gather(bf16[1,1,1,96,128]{4,3,1,0,2:T(8,128)(2,1)} %bitcast.55), channel_id=1, replica_groups=mesh['lag'=4,'row_0'=16,'row_1'=2,'col'=4] {'row_1'}, dimensions={2}, use_global_device_ids=true | all-gather | bytes 73728 | tf_op jit(solution)/shard_map/all_gather | solution.py:13
  10.8 33.4 %all_gather.7 = bf16[1,1,32,96,128]{4,3,1,0,2:T(8,128)(2,1)S(1)} all-gather(bf16[1,1,2,96,128]{4,3,1,0,2:T(8,128)(2,1)S(1)} %all_gather.6), channel_id=1, replica_groups=mesh['lag'=4,'row_0'=16,'row_1'=2,'col'=4] {'row_0'}, dimensions={2}, use_global_device_ids=true | all-gather | bytes 835584 | tf_op jit(solution)/shard_map/all_gather | solution.py:13
  44.2 1.4 fusion.4
  45.6 1.3 fusion.13
  47.0 15.9 %all-to-all-start = ((f32[16,24,128]{2,1,0:T(8,128)}), f32[16,24,128]{2,1,0:T(8,128)S(1)}, u32[]{:S(2)}, u32[]{:S(2)}) async-start(f32[16,24,128]{2,1,0:T(8,128)} %bitcast.4), calls=%async_computation | async-start | bytes 393216 | tf_op jit(solution)/shard_map/all_to_all | solution.py:29
  62.9 0.8 dynamic_slice.40
  63.6 0.8 dynamic_slice.41
  64.4 6.7 %all-to-all-done = f32[16,24,128]{2,1,0:T(8,128)S(1)} async-done(((f32[16,24,128]{2,1,0:T(8,128)}), f32[16,24,128]{2,1,0:T(8,128)S(1)}, u32[]{:S(2)}, u32[]{:S(2)}) %all-to-all-start) | async-done | bytes 196640 | tf_op jit(solution)/shard_map/all_to_all | solution.py:29
  71.2 10.9 %all_to_all.15 = bf16[16,24,128]{2,1,0:T(8,128)(2,1)} all-to-all(bf16[16,24,128]{2,1,0:T(8,128)(2,1)S(1)} %broadcast_in_dim.4), channel_id=1, replica_groups=mesh['lag'=4,'row_0'=16,'row_1'=2,'col'=4] {'lag','col'}, dimensions={0} | all-to-all | bytes 196608 | tf_op jit(solution)/shard_map/all_to_all | solution.py:41
  82.1 2.7 %collective-permute-start = (bf16[3072,128]{1,0:T(8,128)(2,1)S(1)}, bf16[3072,128]{1,0:T(8,128)(2,1)}, u32[]{:S(2)}, u32[]{:S(2)}) collective-permute-start(bf16[3072,128]{1,0:T(8,128)(2,1)S(1)} %bitcast.51), channel_id=1, source_target_pairs={{0,128},{128,256},{256,384},{1,129},{129,257},{257,385},{2,130},{1... | collective-permute-start | bytes 2359304 | tf_op jit(solution)/shard_map/ppermute | solution.py:51
  85.0 104.8 %all-gather.2.cloned.1.call-done = bf16[32,384,128]{2,1,0:T(8,128)(2,1)} async-done(((bf16[1,384,128]{2,1,0:T(8,128)(2,1)}), bf16[32,384,128]{2,1,0:T(8,128)(2,1)}) %all-gather.2.cloned.1.call-update) | async-done | bytes 3145744 | tf_op jit(solution)/shard_map/all_gather | solution.py:18
  189.8 0.9 bitcast_dynamic-update-slice_fusion.7
  190.7 0.9 bitcast_dynamic-update-slice_fusion.6
  191.6 0.9 bitcast_dynamic-update-slice_fusion.5
  192.6 0.9 bitcast_dynamic-update-slice_fusion.4
  193.5 0.9 bitcast_dynamic-update-slice_fusion.3
  194.4 0.9 bitcast_dynamic-update-slice_fusion.2
  195.3 0.9 bitcast_dynamic-update-slice_fusion.1
  196.2 0.9 bitcast_dynamic-update-slice_fusion
  197.1 2.0 fusion.7
  199.2 0.8 dynamic_update_slice.7
  200.1 0.1 copy.11
  200.2 35.6 %all_to_all.16 = f32[16,24,128]{2,1,0:T(8,128)S(1)} all-to-all(f32[16,24,128]{2,1,0:T(8,128)S(1)} %bitcast.53), channel_id=1, replica_groups=mesh['lag'=4,'row_0'=16,'row_1'=2,'col'=4] {'lag','col'}, dimensions={0} | all-to-all | bytes 393216 | tf_op jit(solution)/shard_map/all_to_all | solution.py:29
  235.9 0.6 maximum_bitcast_fusion
  (16 shorter events, 0.5 us)
Async XLA Ops:
  6.5 37.7 %copy-start = (bf16[1,384,3072]{2,1,0:T(8,128)(2,1)S(1)}, bf16[1,384,3072]{2,1,0:T(8,128)(2,1)}, u32[]{:S(2)}) copy-start(bf16[1,384,3072]{2,1,0:T(8,128)(2,1)} %param.5) | copy-start | bytes 7077892
  6.5 39.1 %copy-start.1 = (f32[2,1,1,24,128]{4,3,2,1,0:T(8,128)S(1)}, f32[2,1,1,24,128]{4,3,2,1,0:T(8,128)}, u32[]{:S(2)}) copy-start(f32[2,1,1,24,128]{4,3,2,1,0:T(8,128)} %param.7) | copy-start | bytes 73732
  6.5 78.3 %slice-start = ((f32[2,1,1,24,128]{4,3,2,1,0:T(8,128)}), f32[1,1,1,24,128]{4,3,2,1,0:T(8,128)S(1)}, s32[]{:S(2)}) async-start(f32[2,1,1,24,128]{4,3,2,1,0:T(8,128)} %param.7), calls=%async_computation.4 | async-start | bytes 24576 | tf_op jit(solution)/shard_map/slice | solution.py:78
  47.0 24.1 %all-to-all-start = ((f32[16,24,128]{2,1,0:T(8,128)}), f32[16,24,128]{2,1,0:T(8,128)S(1)}, u32[]{:S(2)}, u32[]{:S(2)}) async-start(f32[16,24,128]{2,1,0:T(8,128)} %bitcast.4), calls=%async_computation | async-start | bytes 393216 | tf_op jit(solution)/shard_map/all_to_all | solution.py:29
  62.8 127.0 %all-gather.2.cloned.1.call-start = ((), (), s32[]{:S(2)}) async-start(), calls=%async_computation.3 | async-start | bytes 3244032 | tf_op jit(solution)/shard_map/all_gather | solution.py:18
  82.1 115.0 %collective-permute-start = (bf16[3072,128]{1,0:T(8,128)(2,1)S(1)}, bf16[3072,128]{1,0:T(8,128)(2,1)}, u32[]{:S(2)}, u32[]{:S(2)}) collective-permute-start(bf16[3072,128]{1,0:T(8,128)(2,1)S(1)} %bitcast.51), channel_id=1, source_target_pairs={{0,128},{128,256},{256,384},{1,129},{129,257},{257,385},{2,130},{1... | collective-permute-start | bytes 2359304 | tf_op jit(solution)/shard_map/ppermute | solution.py:51
Sparse Core Ops, SparseCore 0:
  82.3 107.5 all-gather.1
where the time goes:
time: 244 us; the launch traced here: 243 us
  waiting for transfers between devices  111 us (45%)
  blocking collectives  84.2 us (35%)
  starting transfers between devices  18.6 us (8%)
  between operations  13.6 us (6%)
  local copies, waits for them, and re-layouts  9.88 us (4%)
  matrix products  3.44 us (1%)
    all_gather x1, waiting for transfers between devices, picked(): lax.all_gather(x, axis)  105 us
    all_gather x2, blocking collectives, gather_axes(): x = lax.all_gather(x, axis, axis=dim, tiled=True)  37.7 us
    all_to_all x1, blocking collectives, sum_at_owner(): lax.all_to_all(blocks, axis, split_axis=0, concat_axis=0, tiled=True)  35.6 us
    all_to_all x1, starting transfers between devices, sum_at_owner(): lax.all_to_all(blocks, axis, split_axis=0, concat_axis=0, tiled=True)  15.9 us
    all_to_all x1, blocking collectives, sent_to_all(): return lax.all_to_all(copies, axis, split_axis=0, concat_axis=0, tiled=True)  10.9 us
    all_to_all x1, waiting for transfers between devices, sum_at_owner(): lax.all_to_all(blocks, axis, split_axis=0, concat_axis=0, tiled=True)  6.68 us
    unnamed x12, local copies, waits for them, and re-layouts  6.47 us
  transfers between devices with their start and end apart: 3, of which 2 were waited for; matrix products, arithmetic and copies ran while one was open for 4% of the time, Pallas kernels for 0%

commit v1 on v0

v1 whole, which is shorter than its diff:
```python
import jax
import jax.numpy as jnp
from jax import lax
from jax.sharding import Mesh
from jax.sharding import PartitionSpec as P

STEPS = 2
LAG = ("x_hi", "core")
Z = ("z_hi", "z_lo")
ROW = ("z_hi", "z_lo", "x_lo")
LC = ("x_hi", "core", "y")


def exchange(x, axes):
    return lax.all_to_all(x, axes, split_axis=0, concat_axis=0, tiled=True)


def to_all(x, axes):
    return exchange(jnp.broadcast_to(x, (lax.axis_size(axes), *x.shape)), axes)


def update(residual, inv_rows, coef_rows):
    scaled = residual * inv_rows[:, None]
    return scaled + coef_rows[:, None] * scaled * scaled * scaled


def shards(impedance, history, excitation, inv_self, cubic_coef):
    lag = lax.axis_index(LAG)
    share = lax.axis_index(LC)
    share_rows, width = excitation.shape[3:]
    matrix = impedance[0]
    rows, cols = matrix.shape
    offset = share * share_rows
    inv_rows = lax.dynamic_slice_in_dim(inv_self, offset, share_rows, 0)
    coef_rows = lax.dynamic_slice_in_dim(cubic_coef, offset, share_rows, 0)

    piece = history[0, 0, 0]
    by_z = to_all(piece, Z)
    both = lax.all_gather(by_z, "x_lo", axis=1)
    stored = both.reshape(cols, width)

    def owned(source, moment):
        product = jnp.dot(matrix, source, preferred_element_type=jnp.float32)
        shares = product.reshape(-1, share_rows, width)
        total = exchange(shares, LC).sum(axis=0)
        return update(excitation[moment, 0, 0] - total, inv_rows, coef_rows)

    first = owned(stored, 0)
    shifted = lax.ppermute(stored, LAG, [(k, k + 1) for k in range(3)])
    fresh = to_all(first.astype(jnp.bfloat16), Z)
    n_hi, n_lo, n_x = (lax.axis_size(a) for a in ("z_hi", "z_lo", "x_lo"))
    fresh = fresh.reshape(n_hi, n_lo, share_rows, width)
    n_xhi, n_core, n_y = (lax.axis_size(a) for a in LC)
    planes = jnp.broadcast_to(fresh, (n_xhi, n_x, *fresh.shape))
    planes = planes.reshape(-1, n_lo, share_rows, width)
    planes = exchange(planes, ("x_hi", "x_lo", "y"))
    planes = lax.all_gather(planes, "core")
    planes = planes.reshape(n_core, n_xhi, n_x, n_y, n_lo, share_rows, width)
    block = planes.transpose(4, 2, 1, 0, 3, 5, 6).reshape(cols, width)
    second = owned(jnp.where(lag == 0, block, shifted), 1)
    return jnp.stack([first, second])[:, None, None]


def solution(mesh):
    split = Mesh(
        mesh.devices.reshape(2, 2, 4, 4, 2, 4),
        ("x_hi", "core", "z_hi", "z_lo", "x_lo", "y"),
    )
    in_specs = (
        P(LAG, ROW, "y"),
        P(LAG, "y", ROW, None, None),
        P(None, ROW, LC, None, None),
        P(ROW),
        P(ROW),
    )
    out_specs = P(None, ROW, LC, None, None)
    return jax.shard_map(
        shards, mesh=split, in_specs=in_specs, out_specs=out_specs, check_vma=False
    )
```

time: 244 us -> 122 us (0.50)
  waiting for transfers between devices: 111 us -> 23.7 us
  blocking collectives: 84.2 us -> 58.9 us
  between operations: 13.6 us -> 0.13 us
  starting transfers between devices: 18.6 us -> 29.8 us
  local copies, waits for them, and re-layouts: 9.88 us -> 4.19 us
    all_gather x1 -> x0, waiting for transfers between devices: 105 us -> none  [picked(): lax.all_gather(x, axis)]
    all_gather x2, blocking collectives: 37.7 us -> 13.2 us  [the longest x1 7.41 us: shards(): both = lax.all_gather(by_z, 'x_lo', axis=1)]
    all_to_all x1 -> x3, waiting for transfers between devices: 6.68 us -> 23.7 us  [exchange(): return lax.all_to_all(x, axes, split_axis=0, concat_axis=0, tiled=True)]
    all_to_all x1 -> x3, starting transfers between devices: 15.9 us -> 26.9 us  [exchange(): return lax.all_to_all(x, axes, split_axis=0, concat_axis=0, tiled=True)]
    unnamed x12 -> x10, local copies, waits for them, and re-layouts: 6.47 us -> 0.02 us
  transfers between devices with their start and end apart: 3 -> 4, of which waited for: 2 -> 3; matrix products, arithmetic and copies ran while one was open for 4% -> 2% of each run, Pallas kernels for 0% -> 0%
where the time goes in v1:
time: 122 us; the launch traced here: 121 us
  blocking collectives  58.9 us (48%)
  starting transfers between devices  29.8 us (24%)
  waiting for transfers between devices  23.7 us (19%)
  local copies, waits for them, and re-layouts  4.19 us (3%)
  matrix products  2.31 us (2%)
  other arithmetic  2.04 us (2%)
    all_to_all x2, blocking collectives, exchange(): return lax.all_to_all(x, axes, split_axis=0, concat_axis=0, tiled=True)  45.7 us
    all_to_all x3, starting transfers between devices, exchange(): return lax.all_to_all(x, axes, split_axis=0, concat_axis=0, tiled=True)  26.9 us
    all_to_all x3, waiting for transfers between devices, exchange(): return lax.all_to_all(x, axes, split_axis=0, concat_axis=0, tiled=True)  23.7 us
    all_gather x1, blocking collectives, shards(): both = lax.all_gather(by_z, 'x_lo', axis=1)  7.41 us
    all_gather x1, blocking collectives, shards(): planes = lax.all_gather(planes, 'core')  5.77 us
    ppermute x1, starting transfers between devices, shards(): shifted = lax.ppermute(stored, LAG, [(k, k + 1) for k in range(3)])  2.94 us
  transfers between devices with their start and end apart: 4, of which 3 were waited for; matrix products, arithmetic and copies ran while one was open for 2% of the time, Pallas kernels for 0%

profile of v1, /device:TPU:1, one launch (start us, length us, event | category | flops | bytes accessed | tf_op | source)
XLA Modules:
  0.0 121.0 jit_solution(1675272352494669732)
XLA Ops:
  0.0 0.9 broadcast_in_dim.16
  0.9 33.6 %all_to_all.25 = bf16[16,96,128]{2,1,0:T(8,128)(2,1)S(1)} all-to-all(bf16[16,96,128]{2,1,0:T(8,128)(2,1)S(1)} %broadcast_in_dim.16), channel_id=1, replica_groups=mesh['x_hi'=2,'core'=2,'z_hi'=4,'z_lo'=4,'x_lo'=2,'y'=4] {'z_hi','z_lo'}, dimensions={0} | all-to-all | bytes 786432 | tf_op jit(solution)/shard_map/all_to_all | solution.py:15
  34.6 7.4 %all-gather = bf16[16,192,128]{2,1,0:T(8,128)(2,1)S(1)} all-gather(bf16[16,96,128]{2,1,0:T(8,128)(2,1)S(1)} %all_to_all.25), channel_id=2, replica_groups=mesh['x_hi'=2,'core'=2,'z_hi'=4,'z_lo'=4,'x_lo'=2,'y'=4] {'x_lo'}, dimensions={1}, use_global_device_ids=true | all-gather | bytes 1179648 | tf_op jit(solution)/shard_map/all_gather | solution.py:39
  42.0 1.5 %fusion.9 = f32[16,24,128]{2,1,0:T(8,128)} fusion(bf16[16,24,3072]{2,1,0:T(8,128)(2,1)S(1)} %bitcast.47, bf16[3072,128,1]{1,0,2:T(8,128)(2,1)S(1)} %bitcast.49), kind=kOutput, calls=%fused_computation.15 | convolution fusion | flops 301989888 | bytes 3342336 | tf_op jit(solution)/shard_map/dot_general | solution.py:43
  43.5 14.8 %all-to-all-start.1 = ((f32[16,24,128]{2,1,0:T(8,128)}), f32[16,24,128]{2,1,0:T(8,128)S(1)}, u32[]{:S(2)}, u32[]{:S(2)}) async-start(f32[16,24,128]{2,1,0:T(8,128)} %fusion.9), calls=%async_computation.1 | async-start | bytes 393216 | tf_op jit(solution)/shard_map/all_to_all | solution.py:15
  58.2 0.8 dynamic_slice.7
  59.0 0.8 dynamic_slice.6
  59.7 6.7 %all-to-all-done.1 = f32[16,24,128]{2,1,0:T(8,128)S(1)} async-done(((f32[16,24,128]{2,1,0:T(8,128)}), f32[16,24,128]{2,1,0:T(8,128)S(1)}, u32[]{:S(2)}, u32[]{:S(2)}) %all-to-all-start.1) | async-done | bytes 196640 | tf_op jit(solution)/shard_map/all_to_all | solution.py:15
  66.5 0.1 fusion.5
  66.6 0.7 broadcast_in_dim.17
  67.2 8.6 %all-to-all-start.2 = ((bf16[16,24,128]{2,1,0:T(8,128)(2,1)}), bf16[16,24,128]{2,1,0:T(8,128)(2,1)S(1)}, u32[]{:S(2)}, u32[]{:S(2)}) async-start(bf16[16,24,128]{2,1,0:T(8,128)(2,1)} %broadcast_in_dim.17), calls=%async_computation.2 | async-start | bytes 196608 | tf_op jit(solution)/shard_map/all_to_all | solution.py:15
  75.8 2.9 %collective-permute-start = (bf16[3072,128]{1,0:T(8,128)(2,1)S(1)}, bf16[3072,128]{1,0:T(8,128)(2,1)}, u32[]{:S(2)}, u32[]{:S(2)}) collective-permute-start(bf16[3072,128]{1,0:T(8,128)(2,1)S(1)} %bitcast.50), channel_id=1, source_target_pairs={{0,128},{128,256},{256,384},{1,129},{129,257},{257,385},{2,130},{1... | collective-permute-start | bytes 2359304 | tf_op jit(solution)/shard_map/ppermute | solution.py:49
  78.8 9.0 %all-to-all-done.2 = bf16[16,24,128]{2,1,0:T(8,128)(2,1)S(1)} async-done(((bf16[16,24,128]{2,1,0:T(8,128)(2,1)}), bf16[16,24,128]{2,1,0:T(8,128)(2,1)S(1)}, u32[]{:S(2)}, u32[]{:S(2)}) %all-to-all-start.2) | async-done | bytes 98336 | tf_op jit(solution)/shard_map/all_to_all | solution.py:15
  87.8 0.8 broadcast_in_dim.18
  88.6 3.6 %all-to-all-start.3 = ((bf16[16,4,24,128]{3,2,1,0:T(8,128)(2,1)}), bf16[16,4,24,128]{3,2,1,0:T(8,128)(2,1)S(1)}, u32[]{:S(2)}, u32[]{:S(2)}) async-start(bf16[16,4,24,128]{3,2,1,0:T(8,128)(2,1)} %bitcast.51), calls=%async_computation.3 | async-start | bytes 786432 | tf_op jit(solution)/shard_map/all_to_all | solution.py:15
  92.2 7.9 %all-to-all-done.3 = bf16[16,4,24,128]{3,2,1,0:T(8,128)(2,1)S(1)} async-done(((bf16[16,4,24,128]{3,2,1,0:T(8,128)(2,1)}), bf16[16,4,24,128]{3,2,1,0:T(8,128)(2,1)S(1)}, u32[]{:S(2)}, u32[]{:S(2)}) %all-to-all-start.3) | async-done | bytes 393248 | tf_op jit(solution)/shard_map/all_to_all | solution.py:15
  100.1 5.8 %all-gather.1 = bf16[32,4,24,128]{3,2,1,0:T(8,128)(2,1)S(1)} all-gather(bf16[16,4,24,128]{3,2,1,0:T(8,128)(2,1)S(1)} %all-to-all-done.3), channel_id=3, replica_groups=mesh['x_hi'=2,'core'=2,'z_hi'=4,'z_lo'=4,'x_lo'=2,'y'=4] {'core'}, dimensions={0}, use_global_device_ids=true | all-gather | bytes 1179648 | tf_op jit(solution)/shard_map/all_gather | solution.py:57
  105.9 0.1 copy.8
  106.0 1.2 %bitcast_select_fusion = bf16[3072,128]{1,0:T(8,128)(2,1)S(1)} fusion(bf16[3072,128]{1,0:T(8,128)(2,1)} %collective-permute-done, bf16[4,2,2,2,4,24,128]{6,5,4,3,2,1,0:T(8,128)(2,1)S(1)} %copy.8, pred[]{:T(512)S(6)} %eq.3), kind=kLoop, calls=%fused_computation.3 | loop fusion | flops 393216 | bytes 2359297 | tf_op jit(solution)/shard_map/jit(_where)/select_n | solution.py:60
  107.3 0.8 fusion.2
  108.1 0.1 copy.9
  108.2 12.1 %all_to_all.26 = f32[16,24,128]{2,1,0:T(8,128)S(1)} all-to-all(f32[16,24,128]{2,1,0:T(8,128)S(1)} %bitcast.52), channel_id=1, replica_groups=mesh['x_hi'=2,'core'=2,'z_hi'=4,'z_lo'=4,'x_lo'=2,'y'=4] {'x_hi','core',..., dimensions={0} | all-to-all | bytes 393216 | tf_op jit(solution)/shard_map/all_to_all | solution.py:15
  120.3 0.1 multiply_add_fusion.2
  120.4 0.6 maximum_bitcast_fusion
  (13 shorter events, 0.1 us)
Async XLA Ops:
  0.0 42.0 %copy-start = (bf16[1,384,3072]{2,1,0:T(8,128)(2,1)S(1)}, bf16[1,384,3072]{2,1,0:T(8,128)(2,1)}, u32[]{:S(2)}) copy-start(bf16[1,384,3072]{2,1,0:T(8,128)(2,1)} %param.5) | copy-start | bytes 7077892
  34.6 31.9 %copy-start.1 = (f32[2,1,1,24,128]{4,3,2,1,0:T(8,128)S(1)}, f32[2,1,1,24,128]{4,3,2,1,0:T(8,128)}, u32[]{:S(2)}) copy-start(f32[2,1,1,24,128]{4,3,2,1,0:T(8,128)} %param.7) | copy-start | bytes 73732
  43.5 23.0 %all-to-all-start.1 = ((f32[16,24,128]{2,1,0:T(8,128)}), f32[16,24,128]{2,1,0:T(8,128)S(1)}, u32[]{:S(2)}, u32[]{:S(2)}) async-start(f32[16,24,128]{2,1,0:T(8,128)} %fusion.9), calls=%async_computation.1 | async-start | bytes 393216 | tf_op jit(solution)/shard_map/all_to_all | solution.py:15
  59.7 28.9 %copy-start.3 = (f32[24]{0:T(128)}, f32[24]{0:T(128)S(1)}, u32[]{:S(2)}) copy-start(f32[24]{0:T(128)S(1)} %dynamic_slice.6) | copy-start | bytes 292
  67.2 20.5 %all-to-all-start.2 = ((bf16[16,24,128]{2,1,0:T(8,128)(2,1)}), bf16[16,24,128]{2,1,0:T(8,128)(2,1)S(1)}, u32[]{:S(2)}, u32[]{:S(2)}) async-start(bf16[16,24,128]{2,1,0:T(8,128)(2,1)} %broadcast_in_dim.17), calls=%async_computation.2 | async-start | bytes 196608 | tf_op jit(solution)/shard_map/all_to_all | solution.py:15
  75.8 30.2 %collective-permute-start = (bf16[3072,128]{1,0:T(8,128)(2,1)S(1)}, bf16[3072,128]{1,0:T(8,128)(2,1)}, u32[]{:S(2)}, u32[]{:S(2)}) collective-permute-start(bf16[3072,128]{1,0:T(8,128)(2,1)S(1)} %bitcast.50), channel_id=1, source_target_pairs={{0,128},{128,256},{256,384},{1,129},{129,257},{257,385},{2,130},{1... | collective-permute-start | bytes 2359304 | tf_op jit(solution)/shard_map/ppermute | solution.py:49
  88.6 11.5 %all-to-all-start.3 = ((bf16[16,4,24,128]{3,2,1,0:T(8,128)(2,1)}), bf16[16,4,24,128]{3,2,1,0:T(8,128)(2,1)S(1)}, u32[]{:S(2)}, u32[]{:S(2)}) async-start(bf16[16,4,24,128]{3,2,1,0:T(8,128)(2,1)} %bitcast.51), calls=%async_computation.3 | async-start | bytes 786432 | tf_op jit(solution)/shard_map/all_to_all | solution.py:15
  107.3 13.1 %copy-start.2 = (f32[2,1,1,24,128]{4,3,2,1,0:T(8,128)S(1)}, f32[2,1,1,24,128]{4,3,2,1,0:T(8,128)}, u32[]{:S(2)}) copy-start(f32[2,1,1,24,128]{4,3,2,1,0:T(8,128)} %param.7) | copy-start | bytes 73732
  107.3 13.1 %copy-start.4 = (f32[24]{0:T(128)S(1)}, f32[24]{0:T(128)}, u32[]{:S(2)}) copy-start(f32[24]{0:T(128)} %copy-done.3) | copy-start | bytes 292

commit v2 on v1

--- a/solution.py
+++ b/solution.py
@@ -35,9 +35,8 @@
     coef_rows = lax.dynamic_slice_in_dim(cubic_coef, offset, share_rows, 0)
 
     piece = history[0, 0, 0]
-    by_z = to_all(piece, Z)
-    both = lax.all_gather(by_z, "x_lo", axis=1)
-    stored = both.reshape(cols, width)
+    pair = lax.all_gather(piece, "x_lo")
+    stored = lax.all_gather(pair, Z).reshape(cols, width)
 
     def owned(source, moment):
         product = jnp.dot(matrix, source, preferred_element_type=jnp.float32)

time: 122 us -> 116 us (0.951)
  blocking collectives: 58.9 us -> 55.6 us
    all_to_all x2 -> x1, blocking collectives: 45.7 us -> 12.1 us  [exchange(): return lax.all_to_all(x, axes, split_axis=0, concat_axis=0, tiled=True)]
    all_gather x1 -> x2, blocking collectives: 7.41 us -> 37.8 us  [the longest x1 33.5 us: shards(): stored = lax.all_gather(pair, Z).reshape(cols, width)]
    all_to_all x3, starting transfers between devices: 26.9 us -> 25.6 us  [exchange(): return lax.all_to_all(x, axes, split_axis=0, concat_axis=0, tiled=True)]
where the time goes in v2:
time: 116 us
  blocking collectives  55.6 us (48%)
  starting transfers between devices  28.6 us (25%)
  waiting for transfers between devices  23.7 us (20%)
  local copies, waits for them, and re-layouts  3.25 us (3%)
  matrix products  2.31 us (2%)
  other arithmetic  2.04 us (2%)
    all_gather x1, blocking collectives, shards(): stored = lax.all_gather(pair, Z).reshape(cols, width)  33.5 us
    all_to_all x3, starting transfers between devices, exchange(): return lax.all_to_all(x, axes, split_axis=0, concat_axis=0, tiled=True)  25.6 us
    all_to_all x3, waiting for transfers between devices, exchange(): return lax.all_to_all(x, axes, split_axis=0, concat_axis=0, tiled=True)  23.7 us
    all_to_all x1, blocking collectives, exchange(): return lax.all_to_all(x, axes, split_axis=0, concat_axis=0, tiled=True)  12.1 us
    all_gather x1, blocking collectives, shards(): planes = lax.all_gather(planes, 'core')  5.77 us
    all_gather x1, blocking collectives, shards(): pair = lax.all_gather(piece, 'x_lo')  4.29 us
    ppermute x1, starting transfers between devices, shards(): shifted = lax.ppermute(stored, LAG, [(k, k + 1) for k in range(3)])  2.94 us
  transfers between devices with their start and end apart: 4, of which 3 were waited for; matrix products, arithmetic and copies ran while one was open for 2% of the time, Pallas kernels for 0%

profile of v2, /device:TPU:1, one launch (start us, length us, event | category | flops | bytes accessed | tf_op | source)
XLA Modules:
  0.0 115.6 jit_solution(9903306309999887865)
XLA Ops:
  0.0 4.3 %all-gather = bf16[2,1,1,96,128]{4,3,2,1,0:T(8,128)(2,1)S(1)} all-gather(bf16[1,1,1,96,128]{4,3,2,1,0:T(8,128)(2,1)} %param.6), channel_id=2, replica_groups=mesh['x_hi'=2,'core'=2,'z_hi'=4,'z_lo'=4,'x_lo'=2,'y'=4] {'x_lo'}, dimensions={0}, use_global_device_ids=true | all-gather | bytes 73728 | tf_op jit(solution)/shard_map/all_gather | solution.py:38
  4.3 33.5 %all-gather.1 = bf16[32,1,1,96,128]{4,3,2,1,0:T(8,128)(2,1)S(1)} all-gather(bf16[2,1,1,96,128]{4,3,2,1,0:T(8,128)(2,1)S(1)} %all-gather), channel_id=3, replica_groups=mesh['x_hi'=2,'core'=2,'z_hi'=4,'z_lo'=4,'x_lo'=2,'y'=4] {'z_hi','z_lo'}, dimensions={0}, use_global_device_ids=true | all-gather | bytes 835584 | tf_op jit(solution)/shard_map/all_gather | solution.py:39
  37.8 1.5 %fusion.9 = f32[16,24,128]{2,1,0:T(8,128)} fusion(bf16[16,24,3072]{2,1,0:T(8,128)(2,1)S(1)} %bitcast.46, bf16[3072,128,1]{1,0,2:T(8,128)(2,1)S(1)} %bitcast.48), kind=kOutput, calls=%fused_computation.15 | convolution fusion | flops 301989888 | bytes 3342336 | tf_op jit(solution)/shard_map/dot_general | solution.py:42
  39.3 15.8 %all-to-all-start = ((f32[16,24,128]{2,1,0:T(8,128)}), f32[16,24,128]{2,1,0:T(8,128)S(1)}, u32[]{:S(2)}, u32[]{:S(2)}) async-start(f32[16,24,128]{2,1,0:T(8,128)} %fusion.9), calls=%async_computation | async-start | bytes 393216 | tf_op jit(solution)/shard_map/all_to_all | solution.py:15
  55.1 0.8 dynamic_slice.7
  55.9 0.8 dynamic_slice.6
  56.6 6.7 %all-to-all-done = f32[16,24,128]{2,1,0:T(8,128)S(1)} async-done(((f32[16,24,128]{2,1,0:T(8,128)}), f32[16,24,128]{2,1,0:T(8,128)S(1)}, u32[]{:S(2)}, u32[]{:S(2)}) %all-to-all-start) | async-done | bytes 196640 | tf_op jit(solution)/shard_map/all_to_all | solution.py:15
  63.4 0.1 fusion.5
  63.5 0.7 broadcast_in_dim.6
  64.1 6.2 %all-to-all-start.1 = ((bf16[16,24,128]{2,1,0:T(8,128)(2,1)}), bf16[16,24,128]{2,1,0:T(8,128)(2,1)S(1)}, u32[]{:S(2)}, u32[]{:S(2)}) async-start(bf16[16,24,128]{2,1,0:T(8,128)(2,1)} %broadcast_in_dim.6), calls=%async_computation.1 | async-start | bytes 196608 | tf_op jit(solution)/shard_map/all_to_all | solution.py:15
  70.4 2.9 %collective-permute-start = (bf16[3072,128]{1,0:T(8,128)(2,1)S(1)}, bf16[3072,128]{1,0:T(8,128)(2,1)}, u32[]{:S(2)}, u32[]{:S(2)}) collective-permute-start(bf16[3072,128]{1,0:T(8,128)(2,1)S(1)} %bitcast.49), channel_id=1, source_target_pairs={{0,128},{128,256},{256,384},{1,129},{129,257},{257,385},{2,130},{1... | collective-permute-start | bytes 2359304 | tf_op jit(solution)/shard_map/ppermute | solution.py:48
  73.3 9.0 %all-to-all-done.1 = bf16[16,24,128]{2,1,0:T(8,128)(2,1)S(1)} async-done(((bf16[16,24,128]{2,1,0:T(8,128)(2,1)}), bf16[16,24,128]{2,1,0:T(8,128)(2,1)S(1)}, u32[]{:S(2)}, u32[]{:S(2)}) %all-to-all-start.1) | async-done | bytes 98336 | tf_op jit(solution)/shard_map/all_to_all | solution.py:15
  82.3 0.8 broadcast_in_dim.14
  83.1 3.6 %all-to-all-start.2 = ((bf16[16,4,24,128]{3,2,1,0:T(8,128)(2,1)}), bf16[16,4,24,128]{3,2,1,0:T(8,128)(2,1)S(1)}, u32[]{:S(2)}, u32[]{:S(2)}) async-start(bf16[16,4,24,128]{3,2,1,0:T(8,128)(2,1)} %bitcast.50), calls=%async_computation.2 | async-start | bytes 786432 | tf_op jit(solution)/shard_map/all_to_all | solution.py:15
  86.7 7.9 %all-to-all-done.2 = bf16[16,4,24,128]{3,2,1,0:T(8,128)(2,1)S(1)} async-done(((bf16[16,4,24,128]{3,2,1,0:T(8,128)(2,1)}), bf16[16,4,24,128]{3,2,1,0:T(8,128)(2,1)S(1)}, u32[]{:S(2)}, u32[]{:S(2)}) %all-to-all-start.2) | async-done | bytes 393248 | tf_op jit(solution)/shard_map/all_to_all | solution.py:15
  94.7 5.8 %all-gather.2 = bf16[32,4,24,128]{3,2,1,0:T(8,128)(2,1)S(1)} all-gather(bf16[16,4,24,128]{3,2,1,0:T(8,128)(2,1)S(1)} %all-to-all-done.2), channel_id=4, replica_groups=mesh['x_hi'=2,'core'=2,'z_hi'=4,'z_lo'=4,'x_lo'=2,'y'=4] {'core'}, dimensions={0}, use_global_device_ids=true | all-gather | bytes 1179648 | tf_op jit(solution)/shard_map/all_gather | solution.py:56
  100.4 0.1 copy.8
  100.6 1.2 %bitcast_select_fusion = bf16[3072,128]{1,0:T(8,128)(2,1)S(1)} fusion(bf16[3072,128]{1,0:T(8,128)(2,1)} %collective-permute-done, bf16[4,2,2,2,4,24,128]{6,5,4,3,2,1,0:T(8,128)(2,1)S(1)} %copy.8, pred[]{:T(512)S(6)} %eq.3), kind=kLoop, calls=%fused_computation.3 | loop fusion | flops 393216 | bytes 2359297 | tf_op jit(solution)/shard_map/jit(_where)/select_n | solution.py:59
  101.8 0.0 copy-start.2
  101.8 0.8 fusion.2
  102.7 0.1 copy.9
  102.8 12.1 %all_to_all.20 = f32[16,24,128]{2,1,0:T(8,128)S(1)} all-to-all(f32[16,24,128]{2,1,0:T(8,128)S(1)} %bitcast.51), channel_id=1, replica_groups=mesh['x_hi'=2,'core'=2,'z_hi'=4,'z_lo'=4,'x_lo'=2,'y'=4] {'x_hi','core',..., dimensions={0} | all-to-all | bytes 393216 | tf_op jit(solution)/shard_map/all_to_all | solution.py:15
  114.9 0.1 multiply_add_fusion.2
  115.0 0.6 maximum_bitcast_fusion
  (12 shorter events, 0.1 us)
Async XLA Ops:
  0.0 37.8 %copy-start = (bf16[1,384,3072]{2,1,0:T(8,128)(2,1)S(1)}, bf16[1,384,3072]{2,1,0:T(8,128)(2,1)}, u32[]{:S(2)}) copy-start(bf16[1,384,3072]{2,1,0:T(8,128)(2,1)} %param.5) | copy-start | bytes 7077892
  4.3 59.1 %copy-start.1 = (f32[2,1,1,24,128]{4,3,2,1,0:T(8,128)S(1)}, f32[2,1,1,24,128]{4,3,2,1,0:T(8,128)}, u32[]{:S(2)}) copy-start(f32[2,1,1,24,128]{4,3,2,1,0:T(8,128)} %param.7) | copy-start | bytes 73732
  39.3 24.1 %all-to-all-start = ((f32[16,24,128]{2,1,0:T(8,128)}), f32[16,24,128]{2,1,0:T(8,128)S(1)}, u32[]{:S(2)}, u32[]{:S(2)}) async-start(f32[16,24,128]{2,1,0:T(8,128)} %fusion.9), calls=%async_computation | async-start | bytes 393216 | tf_op jit(solution)/shard_map/all_to_all | solution.py:15
  56.6 26.5 %copy-start.3 = (f32[24]{0:T(128)}, f32[24]{0:T(128)S(1)}, u32[]{:S(2)}) copy-start(f32[24]{0:T(128)S(1)} %dynamic_slice.6) | copy-start | bytes 292
  64.1 18.2 %all-to-all-start.1 = ((bf16[16,24,128]{2,1,0:T(8,128)(2,1)}), bf16[16,24,128]{2,1,0:T(8,128)(2,1)S(1)}, u32[]{:S(2)}, u32[]{:S(2)}) async-start(bf16[16,24,128]{2,1,0:T(8,128)(2,1)} %broadcast_in_dim.6), calls=%async_computation.1 | async-start | bytes 196608 | tf_op jit(solution)/shard_map/all_to_all | solution.py:15
  70.4 30.2 %collective-permute-start = (bf16[3072,128]{1,0:T(8,128)(2,1)S(1)}, bf16[3072,128]{1,0:T(8,128)(2,1)}, u32[]{:S(2)}, u32[]{:S(2)}) collective-permute-start(bf16[3072,128]{1,0:T(8,128)(2,1)S(1)} %bitcast.49), channel_id=1, source_target_pairs={{0,128},{128,256},{256,384},{1,129},{129,257},{257,385},{2,130},{1... | collective-permute-start | bytes 2359304 | tf_op jit(solution)/shard_map/ppermute | solution.py:48
  83.1 11.5 %all-to-all-start.2 = ((bf16[16,4,24,128]{3,2,1,0:T(8,128)(2,1)}), bf16[16,4,24,128]{3,2,1,0:T(8,128)(2,1)S(1)}, u32[]{:S(2)}, u32[]{:S(2)}) async-start(bf16[16,4,24,128]{3,2,1,0:T(8,128)(2,1)} %bitcast.50), calls=%async_computation.2 | async-start | bytes 786432 | tf_op jit(solution)/shard_map/all_to_all | solution.py:15
  101.8 13.1 %copy-start.2 = (f32[2,1,1,24,128]{4,3,2,1,0:T(8,128)S(1)}, f32[2,1,1,24,128]{4,3,2,1,0:T(8,128)}, u32[]{:S(2)}) copy-start(f32[2,1,1,24,128]{4,3,2,1,0:T(8,128)} %param.7) | copy-start | bytes 73732
  101.8 13.1 %copy-start.4 = (f32[24]{0:T(128)S(1)}, f32[24]{0:T(128)}, u32[]{:S(2)}) copy-start(f32[24]{0:T(128)} %copy-done.3) | copy-start | bytes 292

commit v3 on v2

v3 whole, which is shorter than its diff:
```python
import jax
import jax.numpy as jnp
from jax import lax
from jax.experimental import pallas as pl
from jax.experimental.pallas import tpu as pltpu
from jax.experimental.layout import Layout, with_layout_constraint
from jax.sharding import Mesh
from jax.sharding import PartitionSpec as P

LAG = ("x_hi", "core")
Z = ("z_hi", "z_lo")
ROW = ("z_hi", "z_lo", "x_lo")
LC = ("x_hi", "core", "y")
XLC = ("x_lo", "x_hi", "core", "y")


def exchange(x, axes):
    return lax.all_to_all(x, axes, split_axis=0, concat_axis=0, tiled=True)


def to_all(x, axes):
    return exchange(jnp.broadcast_to(x, (lax.axis_size(axes), *x.shape)), axes)


def update(residual, inv_rows, coef_rows):
    scaled = residual * inv_rows[:, None]
    return scaled + coef_rows[:, None] * scaled * scaled * scaled


def turn_kernel(m_ref, o_ref):
    n_x, count, n_z, size, _ = o_ref.shape
    span = count * size
    for j in range(n_x * n_z):
        turned = m_ref[:, j * span : (j + 1) * span].T
        for k in range(count):
            o_ref[j % n_x, k, j // n_x] = turned[k * size : (k + 1) * size]


def turn(matrix, n_x, count, size):
    rows, cols = matrix.shape
    shape = (n_x, count, cols // (n_x * count * size), size, rows)
    return pl.pallas_call(
        turn_kernel,
        in_specs=[pl.BlockSpec(memory_space=pltpu.VMEM)],
        out_specs=pl.BlockSpec(memory_space=pltpu.VMEM),
        out_shape=jax.ShapeDtypeStruct(shape, matrix.dtype),
    )(matrix)


def row_major(x):
    return with_layout_constraint(x, Layout(major_to_minor=tuple(range(x.ndim))))


def shards(impedance, history, excitation, inv_self, cubic_coef):
    share = lax.axis_index(LC)
    share_rows, width = excitation.shape[3:]
    matrix = impedance[0]
    rows, cols = matrix.shape
    offset = share * share_rows
    inv_rows = lax.dynamic_slice_in_dim(inv_self, offset, share_rows, 0)
    coef_rows = lax.dynamic_slice_in_dim(cubic_coef, offset, share_rows, 0)
    n_x, n_y, n_share = (lax.axis_size(a) for a in ("x_lo", "y", LC))

    piece = history[0, 0, 0]
    other = lax.ppermute(piece, "x_lo", [(0, 1), (1, 0)])
    slices = turn(matrix, n_x, n_share, share_rows)
    slices = slices.reshape(n_x * n_share, -1, rows)
    even = lax.axis_index("x_lo") == 0
    pair = jnp.stack([jnp.where(even, piece, other), jnp.where(even, other, piece)])
    slices = exchange(slices, XLC)
    slices = slices.reshape(n_x, n_share, -1, rows)[:, :n_y].reshape(n_x, -1, rows)
    stored = lax.all_gather(pair, Z).reshape(cols, width)

    def owned(shares, axes, moment):
        total = exchange(shares, axes)
        return update(excitation[moment, 0, 0] - total.sum(axis=0), inv_rows, coef_rows)

    shifted = lax.ppermute(stored, LAG, [(k, k + 1) for k in range(3)])
    older = jnp.dot(matrix, shifted, preferred_element_type=jnp.float32)
    older = row_major(lax.optimization_barrier(row_major(older)))
    product = row_major(jnp.dot(matrix, stored, preferred_element_type=jnp.float32))
    first = owned(product.reshape(-1, share_rows, width), LC, 0)
    fresh = to_all(first.astype(jnp.bfloat16), Z).reshape(-1, width)
    newer = jnp.stack(
        [
            lax.dot_general(
                slices[k],
                fresh,
                (((0,), (0,)), ((), ())),
                preferred_element_type=jnp.float32,
            )
            + jnp.where(lax.axis_index("x_lo") == k, older, 0.0)
            for k in range(n_x)
        ]
    )
    second = owned(row_major(newer).reshape(-1, share_rows, width), XLC, 1)
    return jnp.stack([first, second])[:, None, None]


def solution(mesh):
    split = Mesh(
        mesh.devices.reshape(2, 2, 4, 4, 2, 4),
        ("x_hi", "core", "z_hi", "z_lo", "x_lo", "y"),
    )
    in_specs = (
        P(LAG, ROW, "y"),
        P(LAG, "y", ROW, None, None),
        P(None, ROW, LC, None, None),
        P(ROW),
        P(ROW),
    )
    out_specs = P(None, ROW, LC, None, None)
    return jax.shard_map(
        shards, mesh=split, in_specs=in_specs, out_specs=out_specs, check_vma=False
    )
```

time: 116 us -> 141 us (1.22)
  waiting for transfers between devices: 23.7 us -> 39.4 us
  starting transfers between devices: 28.6 us -> 36.1 us
  blocking collectives: 55.6 us -> 50.1 us
  Pallas kernels: 0 us -> 3.74 us
  matrix products: 2.31 us -> 5.61 us
    all_to_all x3, waiting for transfers between devices: 23.7 us -> 38 us  [exchange(): return lax.all_to_all(x, axes, split_axis=0, concat_axis=0, tiled=True)]
    all_gather x2 -> x0, blocking collectives: 10.1 us -> none  [the longest x1 5.77 us: shards(): planes = lax.all_gather(planes, 'core')]
    all_to_all x1, blocking collectives: 12.1 us -> 16.7 us  [exchange(): return lax.all_to_all(x, axes, split_axis=0, concat_axis=0, tiled=True)]
    ppermute x0 -> x1, starting transfers between devices: none -> 3.92 us  [shards(): other = lax.ppermute(piece, 'x_lo', [(0, 1), (1, 0)])]
    pallas_call x0 -> x1, Pallas kernels: none -> 3.74 us  [turn(): pl.pallas_call(turn_kernel, in_specs=[pl.BlockSpec(memory_space=pltpu.VME...]
    dot_general x2 -> x4, matrix products: 2.31 us -> 5.61 us  [the longest x1 3.11 us: shards(): jnp.dot(matrix, stored, preferred_element_type=jnp.float32)]
    ppermute x1, starting transfers between devices: 2.94 us -> 5.07 us  [shards(): shifted = lax.ppermute(stored, LAG, [(k, k + 1) for k in range(3)])]
    all_to_all x3, starting transfers between devices: 25.6 us -> 27.1 us  [exchange(): return lax.all_to_all(x, axes, split_axis=0, concat_axis=0, tiled=True)]
  transfers between devices with their start and end apart: 4 -> 5, of which waited for: 3 -> 4; matrix products, arithmetic and copies ran while one was open for 2% -> 4% of each run, Pallas kernels for 0% -> 3%
where the time goes in v3:
time: 141 us; the launch traced here: 140 us
  blocking collectives  50.1 us (36%)
  waiting for transfers between devices  39.4 us (28%)
  starting transfers between devices  36.1 us (26%)
  matrix products  5.61 us (4%)
  Pallas kernels  3.74 us (3%)
  local copies, waits for them, and re-layouts  3.29 us (2%)
  other arithmetic  1.65 us (1%)
    all_to_all x3, waiting for transfers between devices, exchange(): return lax.all_to_all(x, axes, split_axis=0, concat_axis=0, tiled=True)  38 us
    all_gather x1, blocking collectives, shards(): stored = lax.all_gather(pair, Z).reshape(cols, width)  33.4 us
    all_to_all x3, starting transfers between devices, exchange(): return lax.all_to_all(x, axes, split_axis=0, concat_axis=0, tiled=True)  27.1 us
    all_to_all x1, blocking collectives, exchange(): return lax.all_to_all(x, axes, split_axis=0, concat_axis=0, tiled=True)  16.7 us
    ppermute x1, starting transfers between devices, shards(): shifted = lax.ppermute(stored, LAG, [(k, k + 1) for k in range(3)])  5.07 us
    ppermute x1, starting transfers between devices, shards(): other = lax.ppermute(piece, 'x_lo', [(0, 1), (1, 0)])  3.92 us
    pallas_call x1, Pallas kernels, turn(): pl.pallas_call(turn_kernel, in_specs=[pl.BlockSpec(memory_space=pltpu.VME...  3.74 us
    dot_general x1, matrix products, shards(): jnp.dot(matrix, stored, preferred_element_type=jnp.float32)  3.11 us
  transfers between devices with their start and end apart: 5, of which 4 were waited for; matrix products, arithmetic and copies ran while one was open for 4% of the time, Pallas kernels for 3%

profile of v3, /device:TPU:1, one launch (start us, length us, event | category | flops | bytes accessed | tf_op | source)
XLA Modules:
  0.0 140.0 jit_solution(8915627491034287769)
XLA Ops:
  0.0 3.9 %collective-permute-start = (bf16[96,128]{1,0:T(8,128)(2,1)}, bf16[96,128]{1,0:T(8,128)(2,1)S(1)}, u32[]{:S(2)}, u32[]{:S(2)}) collective-permute-start(bf16[96,128]{1,0:T(8,128)(2,1)} %bitcast.71), channel_id=1, source_target_pairs={{0,4},{4,0},{1,5},{5,1},{2,6},{6,2},{3,7},{7,3},{8,12},{12,8},{9,1... | collective-permute-start | bytes 73736 | tf_op jit(solution)/shard_map/ppermute | solution.py:65
  3.9 1.4 %collective-permute-done = bf16[96,128]{1,0:T(8,128)(2,1)S(1)} collective-permute-done((bf16[96,128]{1,0:T(8,128)(2,1)}, bf16[96,128]{1,0:T(8,128)(2,1)S(1)}, u32[]{:S(2)}, u32[]{:S(2)}) %collective-permute-start) | collective-permute-done | bytes 24608 | tf_op jit(solution)/shard_map/ppermute | solution.py:65
  5.3 0.7 select_bitcast_fusion.1
  6.1 33.4 %all-gather = bf16[32,96,128]{2,1,0:T(8,128)(2,1)S(1)} all-gather(bf16[2,96,128]{2,1,0:T(8,128)(2,1)S(1)} %pad_maximum_fusion.1), channel_id=2, replica_groups=mesh['x_hi'=2,'core'=2,'z_hi'=4,'z_lo'=4,'x_lo'=2,'y'=4] {'z_hi','z_lo'}, dimensions={0}, use_global_device_ids=true | all-gather | bytes 835584 | tf_op jit(solution)/shard_map/all_gather | solution.py:72
  39.5 3.1 %fusion.4 = f32[128,384]{0,1:T(8,128)} fusion(bf16[3072,128]{1,0:T(8,128)(2,1)S(1)} %bitcast.64, bf16[1,384,3072]{2,1,0:T(8,128)(2,1)} %param.5), kind=kOutput, calls=%fused_computation.20 | convolution fusion | flops 301989888 | bytes 3342336 | tf_op jit(solution)/shard_map/dot_general | solution.py:81
  42.6 15.9 %all-to-all-start = ((f32[16,24,128]{2,1,0:T(8,128)}), f32[16,24,128]{2,1,0:T(8,128)S(1)}, u32[]{:S(2)}, u32[]{:S(2)}) async-start(f32[16,24,128]{2,1,0:T(8,128)} %bitcast.7), calls=%async_computation | async-start | bytes 393216 | tf_op jit(solution)/shard_map/all_to_all | solution.py:18
  58.5 3.7 %shard_map.55 = bf16[2,16,4,24,384]{4,3,2,1,0:T(8,128)(2,1)} custom-call(bf16[384,3072]{1,0:T(8,128)(2,1)} %bitcast.62), custom_call_target="tpu_custom_call" | custom-call | tf_op jit(solution)/shard_map/pallas_call | solution.py:42
  62.2 4.5 %all-to-all-done = f32[16,24,128]{2,1,0:T(8,128)S(1)} async-done(((f32[16,24,128]{2,1,0:T(8,128)}), f32[16,24,128]{2,1,0:T(8,128)S(1)}, u32[]{:S(2)}, u32[]{:S(2)}) %all-to-all-start) | async-done | bytes 196640 | tf_op jit(solution)/shard_map/all_to_all | solution.py:18
  66.7 5.0 %all-to-all-start.2 = ((bf16[32,96,384]{2,1,0:T(8,128)(2,1)}), bf16[32,96,384]{2,1,0:T(8,128)(2,1)}, u32[]{:S(2)}, u32[]{:S(2)}) async-start(bf16[32,96,384]{2,1,0:T(8,128)(2,1)} %bitcast.63), calls=%async_computation.2 | async-start | bytes 4718592 | tf_op jit(solution)/shard_map/all_to_all | solution.py:18
  71.7 5.1 %collective-permute-start.1 = (bf16[3072,128]{1,0:T(8,128)(2,1)S(1)}, bf16[3072,128]{1,0:T(8,128)(2,1)}, u32[]{:S(2)}, u32[]{:S(2)}) collective-permute-start(bf16[3072,128]{1,0:T(8,128)(2,1)S(1)} %bitcast.65), channel_id=1, source_target_pairs={{0,128},{128,256},{256,384},{1,129},{129,257},{257,385},{2,130},{1... | collective-permute-start | bytes 2359304 | tf_op jit(solution)/shard_map/ppermute | solution.py:78
  76.8 0.8 dynamic_slice.6
  77.6 0.8 dynamic_slice.7
  78.4 0.1 fusion
  78.4 24.7 %all-to-all-done.2 = bf16[32,96,384]{2,1,0:T(8,128)(2,1)} async-done(((bf16[32,96,384]{2,1,0:T(8,128)(2,1)}), bf16[32,96,384]{2,1,0:T(8,128)(2,1)}, u32[]{:S(2)}, u32[]{:S(2)}) %all-to-all-start.2) | async-done | bytes 2359328 | tf_op jit(solution)/shard_map/all_to_all | solution.py:18
  103.1 0.7 broadcast_in_dim.15
  103.8 6.2 %all-to-all-start.1 = ((bf16[16,24,128]{2,1,0:T(8,128)(2,1)}), bf16[16,24,128]{2,1,0:T(8,128)(2,1)S(1)}, u32[]{:S(2)}, u32[]{:S(2)}) async-start(bf16[16,24,128]{2,1,0:T(8,128)(2,1)} %broadcast_in_dim.15), calls=%async_computation.1 | async-start | bytes 196608 | tf_op jit(solution)/shard_map/all_to_all | solution.py:18
  110.1 1.9 %convolution_bitcast_fusion = f32[384,128]{1,0:T(8,128)S(1)} fusion(bf16[3072,128]{1,0:T(8,128)(2,1)} %collective-permute-done.1, bf16[1,384,3072]{2,1,0:T(8,128)(2,1)S(1)} %copy-done), kind=kOutput, calls=%fused_computation | convolution fusion | flops 301989888 | bytes 3342336 | tf_op jit(solution)/shard_map/dot_general | solution.py:79
  112.0 1.1 fusion.7
  113.1 8.8 %all-to-all-done.1 = bf16[16,24,128]{2,1,0:T(8,128)(2,1)S(1)} async-done(((bf16[16,24,128]{2,1,0:T(8,128)(2,1)}), bf16[16,24,128]{2,1,0:T(8,128)(2,1)S(1)}, u32[]{:S(2)}, u32[]{:S(2)}) %all-to-all-start.1) | async-done | bytes 98336 | tf_op jit(solution)/shard_map/all_to_all | solution.py:18
  121.9 0.3 convolution_bitcast_fusion.2
  122.2 0.3 convolution_bitcast_fusion.1
  122.6 16.7 %all_to_all.20 = f32[32,24,128]{2,1,0:T(8,128)S(1)} all-to-all(f32[32,24,128]{2,1,0:T(8,128)S(1)} %bitcast.66), channel_id=1, replica_groups=mesh['x_hi'=2,'core'=2,'z_hi'=4,'z_lo'=4,'x_lo'=2,'y'=4] {'x_lo','x_hi',..., dimensions={0} | all-to-all | bytes 786432 | tf_op jit(solution)/shard_map/all_to_all | solution.py:18
  139.3 0.1 multiply_add_fusion.2
  139.4 0.6 maximum_bitcast_fusion
  (10 shorter events, 0.1 us)
Async XLA Ops:
  0.0 5.3 %collective-permute-start = (bf16[96,128]{1,0:T(8,128)(2,1)}, bf16[96,128]{1,0:T(8,128)(2,1)S(1)}, u32[]{:S(2)}, u32[]{:S(2)}) collective-permute-start(bf16[96,128]{1,0:T(8,128)(2,1)} %bitcast.71), channel_id=1, source_target_pairs={{0,4},{4,0},{1,5},{5,1},{2,6},{6,2},{3,7},{7,3},{8,12},{12,8},{9,1... | collective-permute-start | bytes 73736 | tf_op jit(solution)/shard_map/ppermute | solution.py:65
  42.6 24.1 %all-to-all-start = ((f32[16,24,128]{2,1,0:T(8,128)}), f32[16,24,128]{2,1,0:T(8,128)S(1)}, u32[]{:S(2)}, u32[]{:S(2)}) async-start(f32[16,24,128]{2,1,0:T(8,128)} %bitcast.7), calls=%async_computation | async-start | bytes 393216 | tf_op jit(solution)/shard_map/all_to_all | solution.py:18
  66.7 11.6 %copy-start.1 = (f32[2,1,1,24,128]{4,3,2,1,0:T(8,128)S(1)}, f32[2,1,1,24,128]{4,3,2,1,0:T(8,128)}, u32[]{:S(2)}) copy-start(f32[2,1,1,24,128]{4,3,2,1,0:T(8,128)} %param.7) | copy-start | bytes 73732
  66.7 43.3 %copy-start = (bf16[1,384,3072]{2,1,0:T(8,128)(2,1)S(1)}, bf16[1,384,3072]{2,1,0:T(8,128)(2,1)}, u32[]{:S(2)}) copy-start(bf16[1,384,3072]{2,1,0:T(8,128)(2,1)} %param.5) | copy-start | bytes 7077892
  66.7 36.4 %all-to-all-start.2 = ((bf16[32,96,384]{2,1,0:T(8,128)(2,1)}), bf16[32,96,384]{2,1,0:T(8,128)(2,1)}, u32[]{:S(2)}, u32[]{:S(2)}) async-start(bf16[32,96,384]{2,1,0:T(8,128)(2,1)} %bitcast.63), calls=%async_computation.2 | async-start | bytes 4718592 | tf_op jit(solution)/shard_map/all_to_all | solution.py:18
  71.7 38.3 %collective-permute-start.1 = (bf16[3072,128]{1,0:T(8,128)(2,1)S(1)}, bf16[3072,128]{1,0:T(8,128)(2,1)}, u32[]{:S(2)}, u32[]{:S(2)}) collective-permute-start(bf16[3072,128]{1,0:T(8,128)(2,1)S(1)} %bitcast.65), channel_id=1, source_target_pairs={{0,128},{128,256},{256,384},{1,129},{129,257},{257,385},{2,130},{1... | collective-permute-start | bytes 2359304 | tf_op jit(solution)/shard_map/ppermute | solution.py:78
  103.8 18.1 %all-to-all-start.1 = ((bf16[16,24,128]{2,1,0:T(8,128)(2,1)}), bf16[16,24,128]{2,1,0:T(8,128)(2,1)S(1)}, u32[]{:S(2)}, u32[]{:S(2)}) async-start(bf16[16,24,128]{2,1,0:T(8,128)(2,1)} %broadcast_in_dim.15), calls=%async_computation.1 | async-start | bytes 196608 | tf_op jit(solution)/shard_map/all_to_all | solution.py:18

commit v4 on v3

--- a/solution.py
+++ b/solution.py
@@ -27,23 +27,49 @@
     return scaled + coef_rows[:, None] * scaled * scaled * scaled
 
 
-def turn_kernel(m_ref, o_ref):
-    n_x, count, n_z, size, _ = o_ref.shape
+def turn_kernel(m_hbm, o_hbm, m_buf, o_buf, in_sem, out_sem):
+    n_x, count, n_z, size, _ = o_buf.shape
     span = count * size
-    for j in range(n_x * n_z):
-        turned = m_ref[:, j * span : (j + 1) * span].T
-        for k in range(count):
-            o_ref[j % n_x, k, j // n_x] = turned[k * size : (k + 1) * size]
+    part = n_x * span
+
+    def read(z):
+        return pltpu.make_async_copy(
+            m_hbm.at[:, z * part : (z + 1) * part], m_buf.at[z], in_sem.at[z]
+        )
+
+    def write(z):
+        return pltpu.make_async_copy(
+            o_buf.at[:, :, z], o_hbm.at[:, :, z], out_sem.at[z]
+        )
+
+    for z in range(n_z):
+        read(z).start()
+    for z in range(n_z):
+        read(z).wait()
+        for x in range(n_x):
+            turned = m_buf[z, :, x * span : (x + 1) * span].T
+            for k in range(count):
+                o_buf[x, k, z] = turned[k * size : (k + 1) * size]
+        write(z).start()
+    for z in range(n_z):
+        write(z).wait()
 
 
 def turn(matrix, n_x, count, size):
     rows, cols = matrix.shape
-    shape = (n_x, count, cols // (n_x * count * size), size, rows)
+    n_z = cols // (n_x * count * size)
+    shape = (n_x, count, n_z, size, rows)
     return pl.pallas_call(
         turn_kernel,
-        in_specs=[pl.BlockSpec(memory_space=pltpu.VMEM)],
-        out_specs=pl.BlockSpec(memory_space=pltpu.VMEM),
+        in_specs=[pl.BlockSpec(memory_space=pl.ANY)],
+        out_specs=pl.BlockSpec(memory_space=pl.ANY),
         out_shape=jax.ShapeDtypeStruct(shape, matrix.dtype),
+        scratch_shapes=[
+            pltpu.VMEM((n_z, rows, cols // n_z), matrix.dtype),
+            pltpu.VMEM(shape, matrix.dtype),
+            pltpu.SemaphoreType.DMA((n_z,)),
+            pltpu.SemaphoreType.DMA((n_z,)),
+        ],
     )(matrix)
 
 
@@ -81,18 +107,14 @@
     product = row_major(jnp.dot(matrix, stored, preferred_element_type=jnp.float32))
     first = owned(product.reshape(-1, share_rows, width), LC, 0)
     fresh = to_all(first.astype(jnp.bfloat16), Z).reshape(-1, width)
-    newer = jnp.stack(
-        [
-            lax.dot_general(
-                slices[k],
-                fresh,
-                (((0,), (0,)), ((), ())),
-                preferred_element_type=jnp.float32,
-            )
-            + jnp.where(lax.axis_index("x_lo") == k, older, 0.0)
-            for k in range(n_x)
-        ]
+    newer = lax.dot_general(
+        slices,
+        jnp.broadcast_to(fresh, (n_x, *fresh.shape)),
+        (((1,), (1,)), ((0,), (0,))),
+        preferred_element_type=jnp.float32,
     )
+    mine = lax.broadcasted_iota(jnp.int32, (n_x, 1, 1), 0) == lax.axis_index("x_lo")
+    newer = newer + jnp.where(mine, older, 0.0)
     second = owned(row_major(newer).reshape(-1, share_rows, width), XLC, 1)
     return jnp.stack([first, second])[:, None, None]
 

time: 141 us -> 140 us (level)
  transfers between devices with their start and end apart: 5 -> 5, of which waited for: 4 -> 4; matrix products, arithmetic and copies ran while one was open for 4% -> 4% of each run, Pallas kernels for 3% -> 2%
where the time goes in v4:
time: 140 us
  blocking collectives  50.1 us (36%)
  waiting for transfers between devices  40.3 us (29%)
  starting transfers between devices  36.1 us (26%)
  matrix products  5.39 us (4%)
  local copies, waits for them, and re-layouts  3.3 us (2%)
  Pallas kernels  2.85 us (2%)
  other arithmetic  1.59 us (1%)
    all_to_all x3, waiting for transfers between devices, exchange(): return lax.all_to_all(x, axes, split_axis=0, concat_axis=0, tiled=True)  38.9 us
    all_gather x1, blocking collectives, shards(): stored = lax.all_gather(pair, Z).reshape(cols, width)  33.4 us
    all_to_all x3, starting transfers between devices, exchange(): return lax.all_to_all(x, axes, split_axis=0, concat_axis=0, tiled=True)  27.1 us
    all_to_all x1, blocking collectives, exchange(): return lax.all_to_all(x, axes, split_axis=0, concat_axis=0, tiled=True)  16.7 us
    ppermute x1, starting transfers between devices, shards(): shifted = lax.ppermute(stored, LAG, [(k, k + 1) for k in range(3)])  5.07 us
    ppermute x1, starting transfers between devices, shards(): other = lax.ppermute(piece, 'x_lo', [(0, 1), (1, 0)])  3.92 us
    dot_general x1, matrix products, shards(): jnp.dot(matrix, stored, preferred_element_type=jnp.float32)  3.11 us
    pallas_call x1, Pallas kernels, turn(): pl.pallas_call(turn_kernel, in_specs=[pl.BlockSpec(memory_space=pl.ANY)],...  2.85 us
  transfers between devices with their start and end apart: 5, of which 4 were waited for; matrix products, arithmetic and copies ran while one was open for 4% of the time, Pallas kernels for 2%

profile of v4, /device:TPU:1, one launch (start us, length us, event | category | flops | bytes accessed | tf_op | source)
XLA Modules:
  0.0 139.7 jit_solution(11225949465898609844)
XLA Ops:
  0.0 3.9 %collective-permute-start = (bf16[96,128]{1,0:T(8,128)(2,1)}, bf16[96,128]{1,0:T(8,128)(2,1)S(1)}, u32[]{:S(2)}, u32[]{:S(2)}) collective-permute-start(bf16[96,128]{1,0:T(8,128)(2,1)} %bitcast.61), channel_id=1, source_target_pairs={{0,4},{4,0},{1,5},{5,1},{2,6},{6,2},{3,7},{7,3},{8,12},{12,8},{9,1... | collective-permute-start | bytes 73736 | tf_op jit(solution)/shard_map/ppermute | solution.py:91
  3.9 1.4 %collective-permute-done = bf16[96,128]{1,0:T(8,128)(2,1)S(1)} collective-permute-done((bf16[96,128]{1,0:T(8,128)(2,1)}, bf16[96,128]{1,0:T(8,128)(2,1)S(1)}, u32[]{:S(2)}, u32[]{:S(2)}) %collective-permute-start) | collective-permute-done | bytes 24608 | tf_op jit(solution)/shard_map/ppermute | solution.py:91
  5.3 0.7 select_bitcast_fusion.1
  6.1 33.4 %all-gather = bf16[32,96,128]{2,1,0:T(8,128)(2,1)S(1)} all-gather(bf16[2,96,128]{2,1,0:T(8,128)(2,1)S(1)} %pad_maximum_fusion), channel_id=2, replica_groups=mesh['x_hi'=2,'core'=2,'z_hi'=4,'z_lo'=4,'x_lo'=2,'y'=4] {'z_hi','z_lo'}, dimensions={0}, use_global_device_ids=true | all-gather | bytes 835584 | tf_op jit(solution)/shard_map/all_gather | solution.py:98
  39.5 3.1 %fusion.7 = f32[128,384]{0,1:T(8,128)} fusion(bf16[3072,128]{1,0:T(8,128)(2,1)S(1)} %bitcast.56, bf16[1,384,3072]{2,1,0:T(8,128)(2,1)} %param.5), kind=kOutput, calls=%fused_computation.19 | convolution fusion | flops 301989888 | bytes 3342336 | tf_op jit(solution)/shard_map/dot_general | solution.py:107
  42.6 15.9 %all-to-all-start = ((f32[16,24,128]{2,1,0:T(8,128)}), f32[16,24,128]{2,1,0:T(8,128)S(1)}, u32[]{:S(2)}, u32[]{:S(2)}) async-start(f32[16,24,128]{2,1,0:T(8,128)} %bitcast.7), calls=%async_computation | async-start | bytes 393216 | tf_op jit(solution)/shard_map/all_to_all | solution.py:18
  58.5 2.9 %shard_map.55 = bf16[2,16,4,24,384]{4,3,2,1,0:T(8,128)(2,1)} custom-call(bf16[384,3072]{1,0:T(8,128)(2,1)} %bitcast.54), custom_call_target="tpu_custom_call" | custom-call | tf_op jit(solution)/shard_map/pallas_call | solution.py:62
  61.3 5.4 %all-to-all-done = f32[16,24,128]{2,1,0:T(8,128)S(1)} async-done(((f32[16,24,128]{2,1,0:T(8,128)}), f32[16,24,128]{2,1,0:T(8,128)S(1)}, u32[]{:S(2)}, u32[]{:S(2)}) %all-to-all-start) | async-done | bytes 196640 | tf_op jit(solution)/shard_map/all_to_all | solution.py:18
  66.7 5.0 %all-to-all-start.2 = ((bf16[32,96,384]{2,1,0:T(8,128)(2,1)}), bf16[32,96,384]{2,1,0:T(8,128)(2,1)}, u32[]{:S(2)}, u32[]{:S(2)}) async-start(bf16[32,96,384]{2,1,0:T(8,128)(2,1)} %bitcast.55), calls=%async_computation.2 | async-start | bytes 4718592 | tf_op jit(solution)/shard_map/all_to_all | solution.py:18
  71.7 5.1 %collective-permute-start.1 = (bf16[3072,128]{1,0:T(8,128)(2,1)S(1)}, bf16[3072,128]{1,0:T(8,128)(2,1)}, u32[]{:S(2)}, u32[]{:S(2)}) collective-permute-start(bf16[3072,128]{1,0:T(8,128)(2,1)S(1)} %bitcast.57), channel_id=1, source_target_pairs={{0,128},{128,256},{256,384},{1,129},{129,257},{257,385},{2,130},{1... | collective-permute-start | bytes 2359304 | tf_op jit(solution)/shard_map/ppermute | solution.py:104
  76.8 0.8 dynamic_slice.7
  77.6 0.8 dynamic_slice.6
  78.4 0.1 fusion.3
  78.4 24.7 %all-to-all-done.2 = bf16[32,96,384]{2,1,0:T(8,128)(2,1)} async-done(((bf16[32,96,384]{2,1,0:T(8,128)(2,1)}), bf16[32,96,384]{2,1,0:T(8,128)(2,1)}, u32[]{:S(2)}, u32[]{:S(2)}) %all-to-all-start.2) | async-done | bytes 2359328 | tf_op jit(solution)/shard_map/all_to_all | solution.py:18
  103.1 0.7 broadcast_in_dim.29
  103.8 6.2 %all-to-all-start.1 = ((bf16[16,24,128]{2,1,0:T(8,128)(2,1)}), bf16[16,24,128]{2,1,0:T(8,128)(2,1)S(1)}, u32[]{:S(2)}, u32[]{:S(2)}) async-start(bf16[16,24,128]{2,1,0:T(8,128)(2,1)} %broadcast_in_dim.29), calls=%async_computation.1 | async-start | bytes 196608 | tf_op jit(solution)/shard_map/all_to_all | solution.py:18
  110.0 0.0 collective-permute-done.1
  110.1 1.9 %convolution_bitcast_fusion.1 = f32[384,128]{1,0:T(8,128)S(1)} fusion(bf16[3072,128]{1,0:T(8,128)(2,1)} %collective-permute-done.1, bf16[1,384,3072]{2,1,0:T(8,128)(2,1)S(1)} %copy-done), kind=kOutput, calls=%fused_computation.1 | convolution fusion | flops 301989888 | bytes 3342336 | tf_op jit(solution)/shard_map/dot_general | solution.py:105
  112.0 1.1 slice.12
  113.1 8.8 %all-to-all-done.1 = bf16[16,24,128]{2,1,0:T(8,128)(2,1)S(1)} async-done(((bf16[16,24,128]{2,1,0:T(8,128)(2,1)}), bf16[16,24,128]{2,1,0:T(8,128)(2,1)S(1)}, u32[]{:S(2)}, u32[]{:S(2)}) %all-to-all-start.1) | async-done | bytes 98336 | tf_op jit(solution)/shard_map/all_to_all | solution.py:18
  121.9 0.4 select_add_fusion
  122.3 16.7 %all_to_all.20 = f32[32,24,128]{2,1,0:T(8,128)S(1)} all-to-all(f32[32,24,128]{2,1,0:T(8,128)S(1)} %bitcast.59), channel_id=1, replica_groups=mesh['x_hi'=2,'core'=2,'z_hi'=4,'z_lo'=4,'x_lo'=2,'y'=4] {'x_lo','x_hi',..., dimensions={0} | all-to-all | bytes 786432 | tf_op jit(solution)/shard_map/all_to_all | solution.py:18
  139.0 0.1 multiply_add_fusion.2
  139.1 0.6 maximum_bitcast_fusion
  (8 shorter events, 0.1 us)
Async XLA Ops:
  0.0 5.3 %collective-permute-start = (bf16[96,128]{1,0:T(8,128)(2,1)}, bf16[96,128]{1,0:T(8,128)(2,1)S(1)}, u32[]{:S(2)}, u32[]{:S(2)}) collective-permute-start(bf16[96,128]{1,0:T(8,128)(2,1)} %bitcast.61), channel_id=1, source_target_pairs={{0,4},{4,0},{1,5},{5,1},{2,6},{6,2},{3,7},{7,3},{8,12},{12,8},{9,1... | collective-permute-start | bytes 73736 | tf_op jit(solution)/shard_map/ppermute | solution.py:91
  42.6 24.1 %all-to-all-start = ((f32[16,24,128]{2,1,0:T(8,128)}), f32[16,24,128]{2,1,0:T(8,128)S(1)}, u32[]{:S(2)}, u32[]{:S(2)}) async-start(f32[16,24,128]{2,1,0:T(8,128)} %bitcast.7), calls=%async_computation | async-start | bytes 393216 | tf_op jit(solution)/shard_map/all_to_all | solution.py:18
  66.7 11.6 %copy-start.1 = (f32[2,1,1,24,128]{4,3,2,1,0:T(8,128)S(1)}, f32[2,1,1,24,128]{4,3,2,1,0:T(8,128)}, u32[]{:S(2)}) copy-start(f32[2,1,1,24,128]{4,3,2,1,0:T(8,128)} %param.7) | copy-start | bytes 73732
  66.7 43.3 %copy-start = (bf16[1,384,3072]{2,1,0:T(8,128)(2,1)S(1)}, bf16[1,384,3072]{2,1,0:T(8,128)(2,1)}, u32[]{:S(2)}) copy-start(bf16[1,384,3072]{2,1,0:T(8,128)(2,1)} %param.5) | copy-start | bytes 7077892
  66.7 36.4 %all-to-all-start.2 = ((bf16[32,96,384]{2,1,0:T(8,128)(2,1)}), bf16[32,96,384]{2,1,0:T(8,128)(2,1)}, u32[]{:S(2)}, u32[]{:S(2)}) async-start(bf16[32,96,384]{2,1,0:T(8,128)(2,1)} %bitcast.55), calls=%async_computation.2 | async-start | bytes 4718592 | tf_op jit(solution)/shard_map/all_to_all | solution.py:18
  71.7 38.3 %collective-permute-start.1 = (bf16[3072,128]{1,0:T(8,128)(2,1)S(1)}, bf16[3072,128]{1,0:T(8,128)(2,1)}, u32[]{:S(2)}, u32[]{:S(2)}) collective-permute-start(bf16[3072,128]{1,0:T(8,128)(2,1)S(1)} %bitcast.57), channel_id=1, source_target_pairs={{0,128},{128,256},{256,384},{1,129},{129,257},{257,385},{2,130},{1... | collective-permute-start | bytes 2359304 | tf_op jit(solution)/shard_map/ppermute | solution.py:104
  103.8 18.1 %all-to-all-start.1 = ((bf16[16,24,128]{2,1,0:T(8,128)(2,1)}), bf16[16,24,128]{2,1,0:T(8,128)(2,1)S(1)}, u32[]{:S(2)}, u32[]{:S(2)}) async-start(bf16[16,24,128]{2,1,0:T(8,128)(2,1)} %broadcast_in_dim.29), calls=%async_computation.1 | async-start | bytes 196608 | tf_op jit(solution)/shard_map/all_to_all | solution.py:18

commit v5 on v4

--- a/solution.py
+++ b/solution.py
@@ -42,17 +42,19 @@
             o_buf.at[:, :, z], o_hbm.at[:, :, z], out_sem.at[z]
         )
 
-    for z in range(n_z):
-        read(z).start()
-    for z in range(n_z):
-        read(z).wait()
-        for x in range(n_x):
-            turned = m_buf[z, :, x * span : (x + 1) * span].T
-            for k in range(count):
-                o_buf[x, k, z] = turned[k * size : (k + 1) * size]
-        write(z).start()
-    for z in range(n_z):
-        write(z).wait()
+    @pl.when(lax.axis_index(LAG) == 0)
+    def _():
+        for z in range(n_z):
+            read(z).start()
+        for z in range(n_z):
+            read(z).wait()
+            for x in range(n_x):
+                turned = m_buf[z, :, x * span : (x + 1) * span].T
+                for k in range(count):
+                    o_buf[x, k, z] = turned[k * size : (k + 1) * size]
+            write(z).start()
+        for z in range(n_z):
+            write(z).wait()
 
 
 def turn(matrix, n_x, count, size):
@@ -92,7 +94,8 @@
     slices = turn(matrix, n_x, n_share, share_rows)
     slices = slices.reshape(n_x * n_share, -1, rows)
     even = lax.axis_index("x_lo") == 0
-    pair = jnp.stack([jnp.where(even, piece, other), jnp.where(even, other, piece)])
+    low, high = jnp.where(even, piece, other), jnp.where(even, other, piece)
+    pair = jnp.concatenate([low, high])
     slices = exchange(slices, XLC)
     slices = slices.reshape(n_x, n_share, -1, rows)[:, :n_y].reshape(n_x, -1, rows)
     stored = lax.all_gather(pair, Z).reshape(cols, width)

time: 140 us -> 140 us (level)
  waiting for transfers between devices: 40.3 us -> 43.1 us
  Pallas kernels: 2.85 us -> 0.07 us
    pallas_call x1, Pallas kernels: 2.85 us -> 0.07 us  [turn(): pl.pallas_call(turn_kernel, in_specs=[pl.BlockSpec(memory_space=pl.ANY)],...]
    all_to_all x3, waiting for transfers between devices: 38.9 us -> 41.6 us  [exchange(): return lax.all_to_all(x, axes, split_axis=0, concat_axis=0, tiled=True)]
  transfers between devices with their start and end apart: 5 -> 5, of which waited for: 4 -> 4; matrix products, arithmetic and copies ran while one was open for 4% -> 4% of each run, Pallas kernels for 2% -> 0%
where the time goes in v5:
time: 140 us
  blocking collectives  50.1 us (36%)
  waiting for transfers between devices  43.1 us (31%)
  starting transfers between devices  36.1 us (26%)
  matrix products  5.39 us (4%)
  local copies, waits for them, and re-layouts  3.3 us (2%)
  other arithmetic  1.59 us (1%)
    all_to_all x3, waiting for transfers between devices, exchange(): return lax.all_to_all(x, axes, split_axis=0, concat_axis=0, tiled=True)  41.6 us
    all_gather x1, blocking collectives, shards(): stored = lax.all_gather(pair, Z).reshape(cols, width)  33.4 us
    all_to_all x3, starting transfers between devices, exchange(): return lax.all_to_all(x, axes, split_axis=0, concat_axis=0, tiled=True)  27.1 us
    all_to_all x1, blocking collectives, exchange(): return lax.all_to_all(x, axes, split_axis=0, concat_axis=0, tiled=True)  16.7 us
    ppermute x1, starting transfers between devices, shards(): shifted = lax.ppermute(stored, LAG, [(k, k + 1) for k in range(3)])  5.07 us
    ppermute x1, starting transfers between devices, shards(): other = lax.ppermute(piece, 'x_lo', [(0, 1), (1, 0)])  3.92 us
    dot_general x1, matrix products, shards(): jnp.dot(matrix, stored, preferred_element_type=jnp.float32)  3.11 us
  transfers between devices with their start and end apart: 5, of which 4 were waited for; matrix products, arithmetic and copies ran while one was open for 4% of the time, Pallas kernels for 0%

profile of v5, /device:TPU:1, one launch (start us, length us, event | category | flops | bytes accessed | tf_op | source)
XLA Modules:
  0.0 139.7 jit_solution(1446464128058750133)
XLA Ops:
  0.0 3.9 %collective-permute-start = (bf16[96,128]{1,0:T(8,128)(2,1)}, bf16[96,128]{1,0:T(8,128)(2,1)S(1)}, u32[]{:S(2)}, u32[]{:S(2)}) collective-permute-start(bf16[96,128]{1,0:T(8,128)(2,1)} %bitcast.54), channel_id=1, source_target_pairs={{0,4},{4,0},{1,5},{5,1},{2,6},{6,2},{3,7},{7,3},{8,12},{12,8},{9,1... | collective-permute-start | bytes 73736 | tf_op jit(solution)/shard_map/ppermute | solution.py:93
  3.9 1.4 %collective-permute-done = bf16[96,128]{1,0:T(8,128)(2,1)S(1)} collective-permute-done((bf16[96,128]{1,0:T(8,128)(2,1)}, bf16[96,128]{1,0:T(8,128)(2,1)S(1)}, u32[]{:S(2)}, u32[]{:S(2)}) %collective-permute-start) | collective-permute-done | bytes 24608 | tf_op jit(solution)/shard_map/ppermute | solution.py:93
  5.3 0.7 broadcast_select_fusion.1
  6.1 33.4 %all-gather = bf16[3072,128]{1,0:T(8,128)(2,1)S(1)} all-gather(bf16[192,128]{1,0:T(8,128)(2,1)S(1)} %pad_maximum_fusion), channel_id=2, replica_groups=mesh['x_hi'=2,'core'=2,'z_hi'=4,'z_lo'=4,'x_lo'=2,'y'=4] {'z_hi','z_lo'}, dimensions={0}, use_global_device_ids=true | all-gather | bytes 835584 | tf_op jit(solution)/shard_map/all_gather | solution.py:101
  39.5 3.1 %fusion.7 = f32[128,384]{0,1:T(8,128)} fusion(bf16[3072,128]{1,0:T(8,128)(2,1)S(1)} %all-gather, bf16[1,384,3072]{2,1,0:T(8,128)(2,1)} %param.5), kind=kOutput, calls=%fused_computation.19 | convolution fusion | flops 301989888 | bytes 3342336 | tf_op jit(solution)/shard_map/dot_general | solution.py:110
  42.6 15.9 %all-to-all-start = ((f32[16,24,128]{2,1,0:T(8,128)}), f32[16,24,128]{2,1,0:T(8,128)S(1)}, u32[]{:S(2)}, u32[]{:S(2)}) async-start(f32[16,24,128]{2,1,0:T(8,128)} %bitcast.4), calls=%async_computation | async-start | bytes 393216 | tf_op jit(solution)/shard_map/all_to_all | solution.py:18
  58.5 0.1 shard_map.55
  58.6 8.2 %all-to-all-done = f32[16,24,128]{2,1,0:T(8,128)S(1)} async-done(((f32[16,24,128]{2,1,0:T(8,128)}), f32[16,24,128]{2,1,0:T(8,128)S(1)}, u32[]{:S(2)}, u32[]{:S(2)}) %all-to-all-start) | async-done | bytes 196640 | tf_op jit(solution)/shard_map/all_to_all | solution.py:18
  66.7 5.0 %all-to-all-start.2 = ((bf16[32,96,384]{2,1,0:T(8,128)(2,1)}), bf16[32,96,384]{2,1,0:T(8,128)(2,1)}, u32[]{:S(2)}, u32[]{:S(2)}) async-start(bf16[32,96,384]{2,1,0:T(8,128)(2,1)} %bitcast.50), calls=%async_computation.2 | async-start | bytes 4718592 | tf_op jit(solution)/shard_map/all_to_all | solution.py:18
  71.7 5.1 %collective-permute-start.1 = (bf16[3072,128]{1,0:T(8,128)(2,1)S(1)}, bf16[3072,128]{1,0:T(8,128)(2,1)}, u32[]{:S(2)}, u32[]{:S(2)}) collective-permute-start(bf16[3072,128]{1,0:T(8,128)(2,1)S(1)} %all-gather), channel_id=1, source_target_pairs={{0,128},{128,256},{256,384},{1,129},{129,257},{257,385},{2,130},{1... | collective-permute-start | bytes 2359304 | tf_op jit(solution)/shard_map/ppermute | solution.py:107
  76.8 0.8 dynamic_slice.7
  77.6 0.8 dynamic_slice.6
  78.4 0.1 fusion.3
  78.4 24.7 %all-to-all-done.2 = bf16[32,96,384]{2,1,0:T(8,128)(2,1)} async-done(((bf16[32,96,384]{2,1,0:T(8,128)(2,1)}), bf16[32,96,384]{2,1,0:T(8,128)(2,1)}, u32[]{:S(2)}, u32[]{:S(2)}) %all-to-all-start.2) | async-done | bytes 2359328 | tf_op jit(solution)/shard_map/all_to_all | solution.py:18
  103.1 0.7 broadcast_in_dim.29
  103.8 6.2 %all-to-all-start.1 = ((bf16[16,24,128]{2,1,0:T(8,128)(2,1)}), bf16[16,24,128]{2,1,0:T(8,128)(2,1)S(1)}, u32[]{:S(2)}, u32[]{:S(2)}) async-start(bf16[16,24,128]{2,1,0:T(8,128)(2,1)} %broadcast_in_dim.29), calls=%async_computation.1 | async-start | bytes 196608 | tf_op jit(solution)/shard_map/all_to_all | solution.py:18
  110.0 0.0 collective-permute-done.1
  110.0 1.9 %convolution_bitcast_fusion.1 = f32[384,128]{1,0:T(8,128)S(1)} fusion(bf16[3072,128]{1,0:T(8,128)(2,1)} %collective-permute-done.1, bf16[1,384,3072]{2,1,0:T(8,128)(2,1)S(1)} %copy-done), kind=kOutput, calls=%fused_computation.1 | convolution fusion | flops 301989888 | bytes 3342336 | tf_op jit(solution)/shard_map/dot_general | solution.py:108
  112.0 1.1 slice.12
  113.1 8.8 %all-to-all-done.1 = bf16[16,24,128]{2,1,0:T(8,128)(2,1)S(1)} async-done(((bf16[16,24,128]{2,1,0:T(8,128)(2,1)}), bf16[16,24,128]{2,1,0:T(8,128)(2,1)S(1)}, u32[]{:S(2)}, u32[]{:S(2)}) %all-to-all-start.1) | async-done | bytes 98336 | tf_op jit(solution)/shard_map/all_to_all | solution.py:18
  121.9 0.4 select_add_fusion
  122.3 16.7 %all_to_all.20 = f32[32,24,128]{2,1,0:T(8,128)S(1)} all-to-all(f32[32,24,128]{2,1,0:T(8,128)S(1)} %bitcast.52), channel_id=1, replica_groups=mesh['x_hi'=2,'core'=2,'z_hi'=4,'z_lo'=4,'x_lo'=2,'y'=4] {'x_lo','x_hi',..., dimensions={0} | all-to-all | bytes 786432 | tf_op jit(solution)/shard_map/all_to_all | solution.py:18
  139.0 0.1 multiply_add_fusion.2
  139.1 0.6 maximum_bitcast_fusion
  (8 shorter events, 0.1 us)
Async XLA Ops:
  0.0 5.3 %collective-permute-start = (bf16[96,128]{1,0:T(8,128)(2,1)}, bf16[96,128]{1,0:T(8,128)(2,1)S(1)}, u32[]{:S(2)}, u32[]{:S(2)}) collective-permute-start(bf16[96,128]{1,0:T(8,128)(2,1)} %bitcast.54), channel_id=1, source_target_pairs={{0,4},{4,0},{1,5},{5,1},{2,6},{6,2},{3,7},{7,3},{8,12},{12,8},{9,1... | collective-permute-start | bytes 73736 | tf_op jit(solution)/shard_map/ppermute | solution.py:93
  42.6 24.1 %all-to-all-start = ((f32[16,24,128]{2,1,0:T(8,128)}), f32[16,24,128]{2,1,0:T(8,128)S(1)}, u32[]{:S(2)}, u32[]{:S(2)}) async-start(f32[16,24,128]{2,1,0:T(8,128)} %bitcast.4), calls=%async_computation | async-start | bytes 393216 | tf_op jit(solution)/shard_map/all_to_all | solution.py:18
  66.7 11.6 %copy-start.1 = (f32[2,1,1,24,128]{4,3,2,1,0:T(8,128)S(1)}, f32[2,1,1,24,128]{4,3,2,1,0:T(8,128)}, u32[]{:S(2)}) copy-start(f32[2,1,1,24,128]{4,3,2,1,0:T(8,128)} %param.7) | copy-start | bytes 73732
  66.7 43.3 %copy-start = (bf16[1,384,3072]{2,1,0:T(8,128)(2,1)S(1)}, bf16[1,384,3072]{2,1,0:T(8,128)(2,1)}, u32[]{:S(2)}) copy-start(bf16[1,384,3072]{2,1,0:T(8,128)(2,1)} %param.5) | copy-start | bytes 7077892
  66.7 36.4 %all-to-all-start.2 = ((bf16[32,96,384]{2,1,0:T(8,128)(2,1)}), bf16[32,96,384]{2,1,0:T(8,128)(2,1)}, u32[]{:S(2)}, u32[]{:S(2)}) async-start(bf16[32,96,384]{2,1,0:T(8,128)(2,1)} %bitcast.50), calls=%async_computation.2 | async-start | bytes 4718592 | tf_op jit(solution)/shard_map/all_to_all | solution.py:18
  71.7 38.3 %collective-permute-start.1 = (bf16[3072,128]{1,0:T(8,128)(2,1)S(1)}, bf16[3072,128]{1,0:T(8,128)(2,1)}, u32[]{:S(2)}, u32[]{:S(2)}) collective-permute-start(bf16[3072,128]{1,0:T(8,128)(2,1)S(1)} %all-gather), channel_id=1, source_target_pairs={{0,128},{128,256},{256,384},{1,129},{129,257},{257,385},{2,130},{1... | collective-permute-start | bytes 2359304 | tf_op jit(solution)/shard_map/ppermute | solution.py:107
  103.8 18.1 %all-to-all-start.1 = ((bf16[16,24,128]{2,1,0:T(8,128)(2,1)}), bf16[16,24,128]{2,1,0:T(8,128)(2,1)S(1)}, u32[]{:S(2)}, u32[]{:S(2)}) async-start(bf16[16,24,128]{2,1,0:T(8,128)(2,1)} %broadcast_in_dim.29), calls=%async_computation.1 | async-start | bytes 196608 | tf_op jit(solution)/shard_map/all_to_all | solution.py:18
